TPU v7x, 256 devices: a whole 4x4x8 slice. The times are simulated.
256 devices in a mesh: copy: 2 (over core), fsdp: 32 (over z, y), tp: 4 (over x).
Axes of the slice: x: 4, y: 4, z: 8, core: 2. Of those that a mesh axis runs over, the one named last changes fastest.
Arguments:
- gradients: float32 [256, 128, 4096], P('copy', 'fsdp', 'tp'), parts along dimension 0, may hold values from -6 to 6
- momentum: float32 [256, 128, 4096], P('copy', 'fsdp', 'tp'), parts along dimension 0, may hold values from -6 to 6
- weights: float32 [256, 128, 4096], P('copy', 'fsdp', 'tp'), parts along dimension 0, may hold values from -0.1875 to 0.1875
Outputs:
- new_weights: float32 [256, 128, 4096], P('copy', 'fsdp', 'tp'), parts along dimension 0
- new_momentum: float32 [256, 128, 4096], P('copy', 'fsdp', 'tp'), parts along dimension 0
There are 2 independent parts, one for each index of `copy`. A program takes and returns all parts, laid end to end along the dimension named above; each array names one. Nothing has to cross between parts.
All inputs are finite; a program needn't handle non-finite values.
Results may differ from a plain program's by a relative error of at most 0.00014.
Values sent between devices are 32-bit elements; how exact they have to be, the bound alone decides.
No kernel may reach another device: no remote copies, remote signals or barrier semaphores. Data moves between devices by JAX's collectives and lax.ppermute only.
A program may use at most 64 MiB of HBM per device.

v0:
```python
import jax
import jax.numpy as jnp
from jax import lax
from jax.sharding import PartitionSpec as P

ITERS = 4


hold_rate = 0.95
learn_rate = 0.9
decay_rate = 0.1


def sent_to_all(x, axis):
    length = lax.axis_size(axis)
    return lax.all_to_all(jnp.broadcast_to(x[None], (length, *x.shape)), axis, 0, 0, tiled=True)


def taken_together(x, axis):
    return sent_to_all(x, axis).sum(axis=0)


def shards(gradients, momentum, weights):
    new_momentum = hold_rate * momentum + gradients
    direction = hold_rate * new_momentum + gradients
    moved = lax.all_to_all(direction, "fsdp", split_axis=0, concat_axis=1, tiled=True)
    total = lax.psum(jnp.sum(moved * moved, axis=(1, 2), keepdims=True), "tp")
    iterate = moved * lax.rsqrt(total + 1e-06)
    for step in range(ITERS):
        gram = taken_together(
            jnp.einsum("mik,mjk->mij", iterate, iterate, precision=lax.Precision.HIGHEST), "tp"
        )
        mixed = -4.775 * gram + 2.0315 * jnp.einsum(
            "mij,mjk->mik", gram, gram, precision=lax.Precision.HIGHEST
        )
        iterate = 3.4445 * iterate + jnp.einsum(
            "mij,mjk->mik", mixed, iterate, precision=lax.Precision.HIGHEST
        )
    back = lax.all_to_all(iterate, "fsdp", split_axis=1, concat_axis=0, tiled=True)
    new_weights = (1.0 - learn_rate * decay_rate) * weights - learn_rate * back
    return (new_weights, new_momentum)


def solution(mesh):
    return jax.shard_map(
        shards,
        mesh=mesh,
        in_specs=(P("copy", "fsdp", "tp"), P("copy", "fsdp", "tp"), P("copy", "fsdp", "tp")),
        out_specs=(P("copy", "fsdp", "tp"), P("copy", "fsdp", "tp")),
        check_vma=False,
    )
```

profile of v0, /device:TPU:8, one launch (start us, length us, event | category | flops | bytes accessed | tf_op | source)
XLA Modules:
  0.0 217.4 jit_solution(7391377207697536260)
XLA Ops:
  0.6 4.6 %multiply_add_fusion.4 = (f32[128,4,1024]{2,1,0:T(4,128)S(1)}, f32[128,4,1024]{2,1,0:T(4,128)}) fusion(f32[128,4,1024]{2,1,0:T(4,128)} %param.3, f32[128,4,1024]{2,1,0:T(4,128)} %param.4), kind=kLoop, calls=%fused_computation.7 | loop fusion | flops 2097152 | bytes 8388608 | tf_op jit(solution)/shard_map/add | solution.py:25
  5.3 62.0 %all_to_all.47 = f32[128,4,1024]{2,1,0:T(4,128)S(1)} all-to-all(f32[128,4,1024]{2,1,0:T(4,128)S(1)} %get-tuple-element.2), channel_id=1, replica_groups=mesh['copy'=2,'fsdp'=32,'tp'=4] {'fsdp'}, dimensions={0} | all-to-all | bytes 4194304 | tf_op jit(solution)/shard_map/all_to_all | solution.py:26
  67.3 0.6 multiply_reduce_fusion
  67.9 10.5 %psum.7 = f32[4,1,1]{0,2,1:T(1,128)S(1)} all-reduce(f32[4,1,1]{0,2,1:T(1,128)S(1)} %bitcast.38), channel_id=1, replica_groups=mesh['copy'=2,'fsdp'=32,'tp'=4] {'tp'}, use_global_device_ids=true, to_apply=%region_1.0 | all-reduce | flops 4 | bytes 32 | tf_op jit(solution)/shard_map/psum | solution.py:27
  78.4 1.5 copy_bitcast_fusion
  79.9 2.0 all_to_all.35
  81.9 2.3 %fusion.2 = f32[4,128,128]{2,1,0:T(8,128)S(1)} fusion(f32[4,128,1024]{2,1,0:T(8,128)S(1)} %all_to_all.35, f32[4]{0:T(128)S(1)} %rsqrt_bitcast_fusion), kind=kOutput, calls=%fused_computation.11 | convolution fusion | flops 805830656 | bytes 2359312 | tf_op jit(solution)/shard_map/mik,mjk->mij/dot_general | solution.py:31
  84.3 14.1 %all_to_all.48 = f32[4,4,128,128]{3,2,1,0:T(8,128)S(1)} all-to-all(f32[4,4,128,128]{3,2,1,0:T(8,128)S(1)} %broadcast_in_dim.11), channel_id=1, replica_groups=mesh['copy'=2,'fsdp'=32,'tp'=4] {'tp'}, dimensions={0} | all-to-all | bytes 2097152 | tf_op jit(solution)/shard_map/all_to_all | solution.py:16
  98.8 4.3 %multiply_add_fusion.3 = f32[4,128,1024]{2,1,0:T(8,128)S(1)} fusion(f32[4,128,1024]{2,1,0:T(8,128)} %copy-done.1, f32[4,128,128]{2,1,0:T(8,128)S(1)} %fusion.9, f32[4]{0:T(128)S(1)} %rsqrt_bitcast_fusion), kind=kOutput, calls=%fused_computation.5 | convolution fusion | flops 807403520 | bytes 4456464 | tf_op jit(solution)/shard_map/mij,mjk->mik/dot_general | solution.py:36
  103.1 2.0 fusion.12
  105.3 13.3 %all_to_all.49 = f32[4,4,128,128]{3,2,1,0:T(8,128)S(1)} all-to-all(f32[4,4,128,128]{3,2,1,0:T(8,128)S(1)} %broadcast_in_dim.12), channel_id=1, replica_groups=mesh['copy'=2,'fsdp'=32,'tp'=4] {'tp'}, dimensions={0} | all-to-all | bytes 2097152 | tf_op jit(solution)/shard_map/all_to_all | solution.py:16
  119.0 2.0 multiply_add_fusion.2
  121.1 2.0 fusion.13
  123.3 13.3 %all_to_all.50 = f32[4,4,128,128]{3,2,1,0:T(8,128)S(1)} all-to-all(f32[4,4,128,128]{3,2,1,0:T(8,128)S(1)} %broadcast_in_dim.13), channel_id=1, replica_groups=mesh['copy'=2,'fsdp'=32,'tp'=4] {'tp'}, dimensions={0} | all-to-all | bytes 2097152 | tf_op jit(solution)/shard_map/all_to_all | solution.py:16
  136.7 0.4 fusion.7
  137.0 4.2 %multiply_add_fusion.1 = f32[4,128,1024]{2,1,0:T(8,128)S(1)} fusion(f32[4,128,1024]{2,1,0:T(8,128)} %copy-done, f32[4,128,128]{2,1,0:T(8,128)S(1)} %fusion.7), kind=kOutput, calls=%fused_computation.3 | convolution fusion | flops 806354944 | bytes 4456448 | tf_op jit(solution)/shard_map/mij,mjk->mik/dot_general | solution.py:36
  141.2 2.0 fusion.14
  143.4 13.3 %all_to_all.51 = f32[4,4,128,128]{3,2,1,0:T(8,128)S(1)} all-to-all(f32[4,4,128,128]{3,2,1,0:T(8,128)S(1)} %broadcast_in_dim.14), channel_id=1, replica_groups=mesh['copy'=2,'fsdp'=32,'tp'=4] {'tp'}, dimensions={0} | all-to-all | bytes 2097152 | tf_op jit(solution)/shard_map/all_to_all | solution.py:16
  157.1 2.0 multiply_add_fusion
  159.2 1.4 copy.11
  160.5 51.9 %all_to_all.52 = f32[4,128,1024]{2,0,1:T(4,128)S(1)} all-to-all(f32[4,128,1024]{2,0,1:T(4,128)S(1)} %copy.11), channel_id=1, replica_groups=mesh['copy'=2,'fsdp'=32,'tp'=4] {'fsdp'}, dimensions={1} | all-to-all | bytes 4194304 | tf_op jit(solution)/shard_map/all_to_all | solution.py:39
  212.4 0.7 broadcast_multiply_fusion
  213.1 1.8 copy.12
  214.9 2.5 %bitcast_subtract_fusion = f32[128,4,1024]{2,1,0:T(4,128)} fusion(f32[32,4,4,1024]{3,2,1,0:T(4,128)S(1)} %copy.12, f32[128,4,1024]{2,1,0:T(4,128)S(1)} %copy-done.2), kind=kLoop, calls=%fused_computation | loop fusion | flops 1048576 | bytes 6291456 | tf_op jit(solution)/shard_map/sub | solution.py:40
  (18 shorter events, 1.8 us)
Async XLA Ops:
  81.9 16.5 %copy-start.1 = (f32[4,128,1024]{2,1,0:T(8,128)}, f32[4,128,1024]{2,1,0:T(8,128)S(1)}, u32[]{:S(2)}) copy-start(f32[4,128,1024]{2,1,0:T(8,128)S(1)} %all_to_all.35) | copy-start | bytes 6291460
  121.1 2.1 copy-start
  213.1 1.8 copy-start.2
where the time goes:
time: 218 us; the launch traced here: 217 us
  blocking collectives  178 us (82%)
  matrix products  22.4 us (10%)
  other arithmetic  8.7 us (4%)
  local copies, waits for them, and re-layouts  7.09 us (3%)
    all_to_all x1, blocking collectives, shards(): lax.all_to_all(direction, 'fsdp', split_axis=0, concat_axis=1, tiled=True)  62 us
    all_to_all x4, blocking collectives, sent_to_all(): lax.all_to_all(jnp.broadcast_to(x[None], (length, *x.shape)), axis, 0, 0,...  54 us
    all_to_all x1, blocking collectives, shards(): lax.all_to_all(iterate, 'fsdp', split_axis=1, concat_axis=0, tiled=True)  51.9 us
    dot_general x4, matrix products, shards(): jnp.einsum('mij,mjk->mik', mixed, iterate, precision=lax.Precision.HIGHEST)  12.5 us
    psum x1, blocking collectives, shards(): total = lax.psum(jnp.sum(moved * moved, axis=(1, 2), keepdims=True), 'tp')  10.5 us
    dot_general x4, matrix products, shards(): jnp.einsum('mik,mjk->mij', iterate, iterate, precision=lax.Precision.HIGH...  8.4 us
    add x1, other arithmetic, shards(): direction = hold_rate * new_momentum + gradients  4.62 us

commit v1 on v0

v1 whole, which is shorter than its diff:
```python
import jax
import jax.numpy as jnp
from jax import lax
from jax.experimental import pallas as pl
from jax.experimental.pallas import tpu as pltpu
from jax.sharding import PartitionSpec as P

ITERS = 4
hold_rate = 0.95
learn_rate = 0.9
decay_rate = 0.1
LINEAR, CUBIC, QUINTIC = 3.4445, -4.775, 2.0315
OWNERS = ("fsdp", "tp")


def dot(a, b, across=False):
    return lax.dot_general(
        a,
        b,
        (((1,), (1 if across else 0,)), ((), ())),
        precision=lax.Precision.HIGHEST,
        preferred_element_type=jnp.float32,
    )


def whole_matrix(x_ref, y_ref):
    sources, lines, lanes = x_ref.shape
    tps = 4
    fsdps = sources // tps
    pairs = lines // 8
    rows = fsdps * 8
    view = x_ref.reshape(fsdps, tps, lines, lanes)
    out = y_ref.reshape(fsdps, tps, lines, lanes)

    def part(t):
        return jnp.concatenate(
            [view[:, t, p * 8 : p * 8 + 8, :].reshape(rows, lanes) for p in range(pairs)], axis=1
        )

    wide = None
    for t in range(tps):
        z = part(t)
        g = dot(z, z, across=True)
        wide = g if wide is None else wide + g
    i = lax.broadcasted_iota(jnp.int32, (rows, rows), 0)
    j = lax.broadcasted_iota(jnp.int32, (rows, rows), 1)
    same_half = ((i // 4) % 2) == ((j // 4) % 2)
    total = jnp.sum(jnp.sum(jnp.where(i == j, wide, 0.0), axis=1, keepdims=True), axis=0, keepdims=True) + 1e-06
    swapped = jnp.where((i // 4) % 2 == 0, pltpu.roll(wide, rows - 4, 0), pltpu.roll(wide, 4, 0))
    swapped = jnp.where((j // 4) % 2 == 0, pltpu.roll(swapped, rows - 4, 1), pltpu.roll(swapped, 4, 1))
    gram = jnp.where(same_half, (wide + swapped) / total, 0.0)
    applied = None
    for step in range(ITERS):
        extra = (CUBIC / LINEAR) * gram + (QUINTIC / LINEAR) * dot(gram, gram)
        applied = extra if applied is None else applied + (extra + dot(extra, applied))
        if step < ITERS - 1:
            gram = LINEAR**2 * (gram + dot(gram, 2.0 * extra + dot(extra, extra)))
    scale = LINEAR**ITERS * lax.rsqrt(total)
    for t in range(tps):
        z = part(t)
        y = scale * (z + dot(applied, z))
        for p in range(pairs):
            out[:, t, p * 8 : p * 8 + 8, :] = y[:, p * lanes : (p + 1) * lanes].reshape(fsdps, 8, lanes)


def by_tile(x):
    mats, rows, columns = x.shape
    return x.reshape(mats, rows, columns // 128, 128).transpose(0, 2, 1, 3).reshape(mats, rows * columns // 128, 128)


def by_row(x, shape):
    mats, rows, columns = shape
    return x.reshape(mats, columns // 128, rows, 128).transpose(0, 2, 1, 3).reshape(shape)


def shards(gradients, momentum, weights):
    shape = gradients.shape
    gradients_t, momentum_t, weights_t = by_tile(gradients), by_tile(momentum), by_tile(weights)
    new_momentum = hold_rate * momentum_t + gradients_t
    direction = hold_rate * new_momentum + gradients_t
    moved = lax.all_to_all(direction, OWNERS, 0, 0, tiled=True)
    iterate = pl.pallas_call(
        whole_matrix,
        out_shape=jax.ShapeDtypeStruct(moved.shape, jnp.float32),
        in_specs=[pl.BlockSpec(memory_space=pltpu.VMEM)],
        out_specs=pl.BlockSpec(memory_space=pltpu.VMEM),
        cost_estimate=pl.CostEstimate(flops=12 * 1000 * 1000 * 1000, bytes_accessed=4 << 20, transcendentals=0),
        compiler_params=pltpu.CompilerParams(vmem_limit_bytes=40 << 20),
        name="whole_matrix",
    )(moved)
    back = lax.all_to_all(iterate, OWNERS, 0, 0, tiled=True)
    new_weights = (1.0 - learn_rate * decay_rate) * weights_t - learn_rate * back
    return by_row(new_weights, shape), by_row(new_momentum, shape)


def solution(mesh):
    spec = P("copy", "fsdp", "tp")
    return jax.shard_map(
        shards, mesh=mesh, in_specs=(spec, spec, spec), out_specs=(spec, spec), check_vma=False
    )
```

time: 218 us -> 150 us (0.69)
  blocking collectives: 178 us -> 67.7 us
  waiting for transfers between devices: 0 us -> 48.3 us
  matrix products: 22.4 us -> 0 us
  Pallas kernels: 0 us -> 13.2 us
  starting transfers between devices: 0 us -> 7.31 us
  local copies, waits for them, and re-layouts: 7.09 us -> 0.01 us
  other arithmetic: 8.7 us -> 12.2 us
    all_to_all x6 -> x1, blocking collectives: 168 us -> 67.7 us  [shards(): moved = lax.all_to_all(direction, OWNERS, 0, 0, tiled=True)]
    all_to_all x0 -> x1, waiting for transfers between devices: none -> 48.3 us  [shards(): back = lax.all_to_all(iterate, OWNERS, 0, 0, tiled=True)]
    dot_general x12 -> x0, matrix products: 22.4 us -> none  [the longest x4 12.5 us: shards(): jnp.einsum('mij,mjk->mik', mixed, iterate, precision=lax.Precision.HIGHEST)]
    pallas_call x0 -> x1, Pallas kernels: none -> 13.2 us  [shards(): pl.pallas_call(whole_matrix, out_shape=jax.ShapeDtypeStruct(moved.shape,...]
    psum x1 -> x0, blocking collectives: 10.5 us -> none  [shards(): total = lax.psum(jnp.sum(moved * moved, axis=(1, 2), keepdims=True), 'tp')]
    all_to_all x0 -> x1, starting transfers between devices: none -> 7.31 us  [shards(): back = lax.all_to_all(iterate, OWNERS, 0, 0, tiled=True)]
    all_to_all x2 -> x0, local copies, waits for them, and re-layouts: 3.52 us -> none  [shards(): lax.all_to_all(direction, 'fsdp', split_axis=0, concat_axis=1, tiled=True)]
    mul x2 -> x1, other arithmetic: 0.69 us -> 3.6 us  [shards(): (1.0 - learn_rate * decay_rate) * weights_t - learn_rate * back]
  transfers between devices with their start and end apart: 0 -> 1, of which waited for: 0 -> 1; matrix products, arithmetic and copies ran while one was open for 0% -> 2% of each run, Pallas kernels for 0% -> 0%
where the time goes in v1:
time: 150 us; the launch traced here: 149 us
  blocking collectives  67.7 us (45%)
  waiting for transfers between devices  48.3 us (32%)
  Pallas kernels  13.2 us (9%)
  other arithmetic  12.2 us (8%)
  starting transfers between devices  7.31 us (5%)
    all_to_all x1, blocking collectives, shards(): moved = lax.all_to_all(direction, OWNERS, 0, 0, tiled=True)  67.7 us
    all_to_all x1, waiting for transfers between devices, shards(): back = lax.all_to_all(iterate, OWNERS, 0, 0, tiled=True)  48.3 us
    pallas_call x1, Pallas kernels, shards(): pl.pallas_call(whole_matrix, out_shape=jax.ShapeDtypeStruct(moved.shape,...  13.2 us
    all_to_all x1, starting transfers between devices, shards(): back = lax.all_to_all(iterate, OWNERS, 0, 0, tiled=True)  7.31 us
    add x1, other arithmetic, shards(): new_momentum = hold_rate * momentum_t + gradients_t  4.74 us
    mul x1, other arithmetic, shards(): (1.0 - learn_rate * decay_rate) * weights_t - learn_rate * back  3.6 us
    sub x1, other arithmetic, shards(): (1.0 - learn_rate * decay_rate) * weights_t - learn_rate * back  3.4 us
  transfers between devices with their start and end apart: 1, of which 1 were waited for; matrix products, arithmetic and copies ran while one was open for 2% of the time, Pallas kernels for 0%

profile of v1, /device:TPU:8, one launch (start us, length us, event | category | flops | bytes accessed | tf_op | source)
XLA Modules:
  0.0 149.4 jit_solution(1251183246714442924)
XLA Ops:
  0.6 0.0 copy-start
  0.6 4.7 %fusion = (f32[128,4,1024]{2,1,0:T(4,128)}, f32[128,4,1024]{2,1,0:T(4,128)S(1)}) fusion(f32[128,4,1024]{2,1,0:T(4,128)} %param.3, f32[128,4,1024]{2,1,0:T(4,128)} %param.4), kind=kLoop, calls=%fused_computation.4 | loop fusion | flops 1048576 | bytes 8388608 | tf_op jit(solution)/shard_map/add | solution.py:79
  5.4 0.0 copy-done
  5.4 0.5 multiply_add_fusion
  5.9 67.7 %all_to_all.10.x_ref = f32[128,32,128]{2,1,0:T(8,128)S(1)} all-to-all(f32[128,32,128]{2,1,0:T(8,128)S(1)} %multiply_add_fusion), channel_id=1, replica_groups=mesh['copy'=2,'fsdp'=32,'tp'=4] {'fsdp','tp'}, dimensions={0} | all-to-all | bytes 4194304 | tf_op jit(solution)/shard_map/all_to_all | solution.py:81
  73.6 13.2 %whole_matrix.1 = f32[128,32,128]{2,1,0:T(8,128)} custom-call(f32[128,32,128]{2,1,0:T(8,128)S(1)} %all_to_all.10.x_ref), custom_call_target="tpu_custom_call" | custom-call | flops 12000000000 | bytes 4194304 | tf_op jit(solution)/shard_map/whole_matrix/pallas_call | solution.py:82
  86.8 7.3 %all-to-all-start.1 = ((f32[128,32,128]{2,1,0:T(8,128)}), f32[128,32,128]{2,1,0:T(8,128)S(1)}, u32[]{:S(2)}, u32[]{:S(2)}) async-start(f32[128,32,128]{2,1,0:T(8,128)} %whole_matrix.1), calls=%async_computation.1 | async-start | bytes 4194304 | tf_op jit(solution)/shard_map/all_to_all | solution.py:91
  94.1 3.6 %broadcast_multiply_fusion.1 = f32[128,4,1024]{2,1,0:T(4,128)} fusion(f32[128,4,1024]{2,1,0:T(4,128)} %param.5), kind=kLoop, calls=%fused_computation.3 | loop fusion | flops 524288 | bytes 4194304 | tf_op jit(solution)/shard_map/mul | solution.py:92
  97.7 48.3 %all-to-all-done.1 = f32[128,32,128]{2,1,0:T(8,128)S(1)} async-done(((f32[128,32,128]{2,1,0:T(8,128)}), f32[128,32,128]{2,1,0:T(8,128)S(1)}, u32[]{:S(2)}, u32[]{:S(2)}) %all-to-all-start.1) | async-done | bytes 2097184 | tf_op jit(solution)/shard_map/all_to_all | solution.py:91
  146.0 3.4 %multiply_subtract_fusion = f32[128,32,128]{2,1,0:T(8,128)} fusion(f32[128,32,128]{2,1,0:T(8,128)} %bitcast.20, f32[128,32,128]{2,1,0:T(8,128)S(1)} %all-to-all-done.1), kind=kLoop, calls=%fused_computation | loop fusion | flops 1048576 | bytes 6291456 | tf_op jit(solution)/shard_map/sub | solution.py:92
Async XLA Ops:
  0.6 4.8 %copy-start = (f32[128,4,1024]{2,1,0:T(4,128)S(1)}, f32[128,4,1024]{2,1,0:T(4,128)}, u32[]{:S(2)}) copy-start(f32[128,4,1024]{2,1,0:T(4,128)} %param.3) | copy-start | bytes 6291460
  86.8 59.2 %all-to-all-start.1 = ((f32[128,32,128]{2,1,0:T(8,128)}), f32[128,32,128]{2,1,0:T(8,128)S(1)}, u32[]{:S(2)}, u32[]{:S(2)}) async-start(f32[128,32,128]{2,1,0:T(8,128)} %whole_matrix.1), calls=%async_computation.1 | async-start | bytes 4194304 | tf_op jit(solution)/shard_map/all_to_all | solution.py:91

commit v2 on v1

--- a/solution.py
+++ b/solution.py
@@ -11,6 +11,7 @@
 decay_rate = 0.1
 LINEAR, CUBIC, QUINTIC = 3.4445, -4.775, 2.0315
 OWNERS = ("fsdp", "tp")
+TURN_NANOS = 22000
 
 
 def dot(a, b, across=False):
@@ -55,12 +56,28 @@
         applied = extra if applied is None else applied + (extra + dot(extra, applied))
         if step < ITERS - 1:
             gram = LINEAR**2 * (gram + dot(gram, 2.0 * extra + dot(extra, extra)))
-    scale = LINEAR**ITERS * lax.rsqrt(total)
+    scale = learn_rate * LINEAR**ITERS * lax.rsqrt(total)
     for t in range(tps):
         z = part(t)
         y = scale * (z + dot(applied, z))
         for p in range(pairs):
             out[:, t, p * 8 : p * 8 + 8, :] = y[:, p * lanes : (p + 1) * lanes].reshape(fsdps, 8, lanes)
+
+
+def hold(nanos_ref, x_ref, same_ref):
+    pl.delay(nanos_ref[0])
+
+
+def after_turn(x, nanos):
+    return pl.pallas_call(
+        hold,
+        out_shape=jax.ShapeDtypeStruct(x.shape, x.dtype),
+        in_specs=[pl.BlockSpec(memory_space=pltpu.SMEM), pl.BlockSpec(memory_space=pl.ANY)],
+        out_specs=pl.BlockSpec(memory_space=pl.ANY),
+        input_output_aliases={1: 0},
+        compiler_params=pltpu.CompilerParams(vmem_limit_bytes=1 << 20),
+        name="hold",
+    )(((1 - lax.axis_index("copy")) * nanos).reshape(1), x)
 
 
 def by_tile(x):
@@ -75,9 +92,10 @@
 
 def shards(gradients, momentum, weights):
     shape = gradients.shape
-    gradients_t, momentum_t, weights_t = by_tile(gradients), by_tile(momentum), by_tile(weights)
-    new_momentum = hold_rate * momentum_t + gradients_t
-    direction = hold_rate * new_momentum + gradients_t
+    direction = by_tile(hold_rate * (hold_rate * momentum + gradients) + gradients)
+    direction = after_turn(direction, TURN_NANOS)
+    gradients, momentum = lax.optimization_barrier((gradients, momentum))
+    new_momentum = hold_rate * momentum + gradients
     moved = lax.all_to_all(direction, OWNERS, 0, 0, tiled=True)
     iterate = pl.pallas_call(
         whole_matrix,
@@ -89,8 +107,8 @@
         name="whole_matrix",
     )(moved)
     back = lax.all_to_all(iterate, OWNERS, 0, 0, tiled=True)
-    new_weights = (1.0 - learn_rate * decay_rate) * weights_t - learn_rate * back
-    return by_row(new_weights, shape), by_row(new_momentum, shape)
+    new_weights = (1.0 - learn_rate * decay_rate) * weights - by_row(back, shape)
+    return new_weights, new_momentum
 
 
 def solution(mesh):

time: 150 us -> 130 us (0.87)
  waiting for transfers between devices: 48.3 us -> 27.3 us
    all_to_all x1, waiting for transfers between devices: 48.3 us -> 27.3 us  [shards(): back = lax.all_to_all(iterate, OWNERS, 0, 0, tiled=True)]
    mul x1 -> x0, other arithmetic: 3.6 us -> none  [shards(): (1.0 - learn_rate * decay_rate) * weights_t - learn_rate * back]
    add x2, other arithmetic: 5.25 us -> 7.22 us  [the longest x1 3.94 us: shards(): new_momentum = hold_rate * momentum + gradients]
  transfers between devices with their start and end apart: 1 -> 1, of which waited for: 1 -> 1; matrix products, arithmetic and copies ran while one was open for 2% -> 3% of each run, Pallas kernels for 0% -> 0%
where the time goes in v2:
time: 130 us; the launch traced here: 129 us
  blocking collectives  68.8 us (53%)
  waiting for transfers between devices  27.3 us (21%)
  Pallas kernels  13.2 us (10%)
  other arithmetic  11.8 us (9%)
  starting transfers between devices  7.63 us (6%)
    all_to_all x1, blocking collectives, shards(): moved = lax.all_to_all(direction, OWNERS, 0, 0, tiled=True)  68.8 us
    all_to_all x1, waiting for transfers between devices, shards(): back = lax.all_to_all(iterate, OWNERS, 0, 0, tiled=True)  27.3 us
    pallas_call x1, Pallas kernels, shards(): pl.pallas_call(whole_matrix, out_shape=jax.ShapeDtypeStruct(moved.shape,...  13.2 us
    all_to_all x1, starting transfers between devices, shards(): back = lax.all_to_all(iterate, OWNERS, 0, 0, tiled=True)  7.63 us
    sub x1, other arithmetic, shards(): (1.0 - learn_rate * decay_rate) * weights - by_row(back, shape)  4.57 us
    add x1, other arithmetic, shards(): new_momentum = hold_rate * momentum + gradients  3.94 us
    add x1, other arithmetic, shards(): hold_rate * (hold_rate * momentum + gradients) + gradients  3.28 us
  transfers between devices with their start and end apart: 1, of which 1 were waited for; matrix products, arithmetic and copies ran while one was open for 3% of the time, Pallas kernels for 0%

profile of v2, /device:TPU:8, one launch (start us, length us, event | category | flops | bytes accessed | tf_op | source)
XLA Modules:
  0.0 129.4 jit_solution(10134089190736506965)
XLA Ops:
  0.6 3.3 %multiply_add_fusion.1 = f32[128,4,1024]{2,1,0:T(4,128)S(1)} fusion(f32[128,4,1024]{2,1,0:T(4,128)} %param.3, f32[128,4,1024]{2,1,0:T(4,128)} %param.4), kind=kLoop, calls=%fused_computation.1 | loop fusion | flops 2097152 | bytes 6291456 | tf_op jit(solution)/shard_map/add | solution.py:95
  3.9 68.8 %all_to_all.10.x_ref = f32[128,32,128]{2,1,0:T(8,128)S(1)} all-to-all(f32[128,32,128]{2,1,0:T(8,128)S(1)} %hold.1), channel_id=1, replica_groups=mesh['copy'=2,'fsdp'=32,'tp'=4] {'fsdp','tp'}, dimensions={0} | all-to-all | bytes 4194304 | tf_op jit(solution)/shard_map/all_to_all | solution.py:99
  72.8 13.2 %whole_matrix.1 = f32[128,32,128]{2,1,0:T(8,128)} custom-call(f32[128,32,128]{2,1,0:T(8,128)S(1)} %all_to_all.10.x_ref), custom_call_target="tpu_custom_call" | custom-call | flops 12000000000 | bytes 4194304 | tf_op jit(solution)/shard_map/whole_matrix/pallas_call | solution.py:100
  85.9 0.0 copy-start
  85.9 7.6 %all-to-all-start.1 = ((f32[128,32,128]{2,1,0:T(8,128)}), f32[128,32,128]{2,1,0:T(8,128)}, u32[]{:S(2)}, u32[]{:S(2)}) async-start(f32[128,32,128]{2,1,0:T(8,128)} %whole_matrix.1), calls=%async_computation.1 | async-start | bytes 4194304 | tf_op jit(solution)/shard_map/all_to_all | solution.py:109
  93.6 0.0 copy-done
  93.6 3.9 %multiply_add_fusion = f32[128,4,1024]{2,1,0:T(4,128)} fusion(f32[128,4,1024]{2,1,0:T(4,128)S(1)} %copy-done, f32[128,4,1024]{2,1,0:T(4,128)} %param.4), kind=kLoop, calls=%fused_computation | loop fusion | flops 1048576 | bytes 6291456 | tf_op jit(solution)/shard_map/add | solution.py:98
  97.5 27.3 %all-to-all-done.1 = f32[128,32,128]{2,1,0:T(8,128)} async-done(((f32[128,32,128]{2,1,0:T(8,128)}), f32[128,32,128]{2,1,0:T(8,128)}, u32[]{:S(2)}, u32[]{:S(2)}) %all-to-all-start.1) | async-done | bytes 2097184 | tf_op jit(solution)/shard_map/all_to_all | solution.py:109
  124.8 4.6 %multiply_subtract_fusion = f32[128,4,1024]{2,1,0:T(4,128)} fusion(f32[128,4,1024]{2,1,0:T(4,128)} %bitcast.6, f32[128,4,1024]{2,1,0:T(4,128)} %param.5), kind=kLoop, calls=%fused_computation.2 | loop fusion | flops 1048576 | bytes 6291456 | tf_op jit(solution)/shard_map/sub | solution.py:110
  (1 shorter events, 0.0 us)
Async XLA Ops:
  85.9 7.6 %copy-start = (f32[128,4,1024]{2,1,0:T(4,128)S(1)}, f32[128,4,1024]{2,1,0:T(4,128)}, u32[]{:S(2)}) copy-start(f32[128,4,1024]{2,1,0:T(4,128)} %param.3) | copy-start | bytes 6291460
  85.9 38.9 %all-to-all-start.1 = ((f32[128,32,128]{2,1,0:T(8,128)}), f32[128,32,128]{2,1,0:T(8,128)}, u32[]{:S(2)}, u32[]{:S(2)}) async-start(f32[128,32,128]{2,1,0:T(8,128)} %whole_matrix.1), calls=%async_computation.1 | async-start | bytes 4194304 | tf_op jit(solution)/shard_map/all_to_all | solution.py:109

commit v3 on v1

v3 whole, which is shorter than its diff:
```python
import jax
import jax.numpy as jnp
from jax import lax
from jax.experimental import pallas as pl
from jax.experimental.pallas import tpu as pltpu
from jax.sharding import PartitionSpec as P

ITERS = 4
hold_rate = 0.95
learn_rate = 0.9
decay_rate = 0.1
LINEAR, CUBIC, QUINTIC = 3.4445, -4.775, 2.0315
OWNERS = ("fsdp", "tp")
TURN_NANOS = 18000


def dot(a, b, across=False):
    return lax.dot_general(
        a, b, (((1,), (1 if across else 0,)), ((), ())), preferred_element_type=jnp.float32
    )


def pieces(x):
    high = x.astype(jnp.bfloat16)
    rest = x - high.astype(jnp.float32)
    middle = rest.astype(jnp.bfloat16)
    return high, middle, (rest - middle.astype(jnp.float32)).astype(jnp.bfloat16)


def left_factors(a):
    high, middle, low = pieces(a)
    first = jnp.concatenate([high, middle], axis=1)
    second = jnp.concatenate([middle, high], axis=1)
    return jnp.concatenate([first, second], axis=0), jnp.concatenate([low, high], axis=1)


def times(factors, high, middle, low):
    main, rest = factors
    rows = rest.shape[0]
    y = dot(main, jnp.concatenate([high, middle], axis=0))
    return (y[:rows] + y[rows:]) + dot(rest, jnp.concatenate([high, low], axis=0))


def product(a, b):
    return times(left_factors(a), *pieces(b))


def whole_matrix(x_ref, y_ref, main_ref, low_ref):
    sources, lines, lanes = x_ref.shape
    rows = low_ref.shape[0]
    tps = sources * 4 // rows
    fsdps = sources // tps
    view = x_ref.reshape(fsdps, tps, lines, lanes)
    out = y_ref.reshape(fsdps, tps, lines, lanes)
    upper = lax.broadcasted_iota(jnp.int32, (fsdps // 2, 8, lanes), 1) < 4
    places = [(t, p, (t * (lines // 8) + p) * 2 * lanes) for t in range(tps) for p in range(lines // 8)]

    def cross(a, b):
        return jnp.where(upper, a, pltpu.roll(b, 4, 1)), jnp.where(upper, pltpu.roll(a, 4, 1), b)

    def columns(t, p):
        z = view[:, t, p * 8 : p * 8 + 8, :].reshape(fsdps // 2, 2, 8, lanes)
        left, right = cross(z[:, 0], z[:, 1])
        return jnp.concatenate([left.reshape(rows, lanes), right.reshape(rows, lanes)], axis=1)

    for t, p, c in places:
        high, middle, low = pieces(columns(t, p))
        main_ref[:rows, c : c + 2 * lanes] = high
        main_ref[rows:, c : c + 2 * lanes] = middle
        low_ref[:, c : c + 2 * lanes] = low
    square = dot(main_ref[...], main_ref[...], across=True)
    mixed = dot(main_ref[:rows], low_ref[...], across=True)
    gram = (
        (square[:rows, :rows] + square[rows:, rows:])
        + (square[:rows, rows:] + square[rows:, :rows])
        + (mixed + mixed.T)
    )
    i = lax.broadcasted_iota(jnp.int32, (rows, rows), 0)
    j = lax.broadcasted_iota(jnp.int32, (rows, rows), 1)
    total = jnp.sum(jnp.sum(jnp.where(i == j, gram, 0.0), axis=1, keepdims=True), axis=0, keepdims=True) + 1e-06
    gram = gram / total
    applied = None
    for step in range(ITERS):
        factors = left_factors(gram)
        extra = (CUBIC / LINEAR) * gram + (QUINTIC / LINEAR) * times(factors, *pieces(gram))
        applied = extra if applied is None else applied + (extra + product(extra, applied))
        if step < ITERS - 1:
            gram = LINEAR**2 * (gram + times(factors, *pieces(2.0 * extra + product(extra, extra))))
    scale = learn_rate * LINEAR**ITERS * lax.rsqrt(total)
    factors = left_factors(applied)
    for t, p, c in places:
        span = slice(c, c + 2 * lanes)
        y = scale * (columns(t, p) + times(factors, main_ref[:rows, span], main_ref[rows:, span], low_ref[:, span]))
        left, right = (y[:, :lanes].reshape(fsdps // 2, 8, lanes), y[:, lanes:].reshape(fsdps // 2, 8, lanes))
        a, b = cross(left, right)
        z = jnp.concatenate([a[:, None], b[:, None]], axis=1).reshape(fsdps, 8, lanes)
        out[:, t, p * 8 : p * 8 + 8, :] = z


CHUNKS = 8


def chunk(c, size):
    return pl.ds(c * (size // CHUNKS), size // CHUNKS)


def stepped(momentum, gradients):
    return hold_rate * momentum + gradients


def first_part(waits_ref, momentum_ref, gradients_ref, direction_ref, new_momentum_ref, m, g, n, reads, writes):
    mats = m.shape[0]

    def read(c, hbm, vmem, k):
        return pltpu.make_async_copy(hbm.at[chunk(c, mats)], vmem.at[chunk(c, mats)], reads.at[k, c])

    def write(c):
        return pltpu.make_async_copy(n.at[chunk(c, mats)], new_momentum_ref.at[chunk(c, mats)], writes.at[c])

    for c in range(CHUNKS):
        read(c, momentum_ref, m, 0).start()
        read(c, gradients_ref, g, 1).start()
    for c in range(CHUNKS):
        read(c, momentum_ref, m, 0).wait()
        read(c, gradients_ref, g, 1).wait()
        at = chunk(c, mats)
        direction_ref[at] = hold_rate * stepped(m[at], g[at]) + g[at]

    @pl.when(waits_ref[0] > 0)
    def _():
        for c in range(CHUNKS):
            at = chunk(c, mats)
            n[at] = stepped(m[at], g[at])
            write(c).start()
        for c in range(CHUNKS):
            write(c).wait()
        pl.delay(waits_ref[0])


def last_part(waits_ref, weights_ref, back_ref, momentum_ref, gradients_ref, kept_ref, new_weights_ref, new_momentum_ref, w, n, writes):
    mats = w.shape[0]

    def write(c, vmem, hbm, k):
        return pltpu.make_async_copy(vmem.at[chunk(c, mats)], hbm.at[chunk(c, mats)], writes.at[k, c])

    for c in range(CHUNKS):
        at = chunk(c, mats)
        w[at] = (1.0 - learn_rate * decay_rate) * weights_ref[at] - back_ref[at]
        write(c, w, new_weights_ref, 0).start()

    @pl.when(waits_ref[0] == 0)
    def _():
        for c in range(CHUNKS):
            at = chunk(c, mats)
            n[at] = stepped(momentum_ref[at], gradients_ref[at])
            write(c, n, new_momentum_ref, 1).start()
        for c in range(CHUNKS):
            write(c, n, new_momentum_ref, 1).wait()

    for c in range(CHUNKS):
        write(c, w, new_weights_ref, 0).wait()


def by_tile(x):
    mats, rows, columns = x.shape
    return x.reshape(mats, rows, columns // 128, 128).transpose(0, 2, 1, 3).reshape(mats, rows * columns // 128, 128)


def by_row(x, shape):
    mats, rows, columns = shape
    return x.reshape(mats, columns // 128, rows, 128).transpose(0, 2, 1, 3).reshape(shape)


def shards(gradients, momentum, weights):
    shape = gradients.shape
    rows = shape[1] * lax.axis_size("fsdp")
    columns = shape[2] * lax.axis_size("tp")
    gradients, momentum, weights = by_tile(gradients), by_tile(momentum), by_tile(weights)
    like = jax.ShapeDtypeStruct(gradients.shape, jnp.float32)
    held = pltpu.VMEM(gradients.shape, jnp.float32)
    in_vmem, in_smem, in_hbm = (pl.BlockSpec(memory_space=m) for m in (pltpu.VMEM, pltpu.SMEM, pltpu.HBM))
    waits = ((1 - lax.axis_index("copy")) * TURN_NANOS).reshape(1)
    direction, new_momentum = pl.pallas_call(
        first_part,
        out_shape=(like, like),
        in_specs=[in_smem, in_hbm, in_hbm],
        out_specs=(in_vmem, in_hbm),
        scratch_shapes=[held, held, held, pltpu.SemaphoreType.DMA((2, CHUNKS)), pltpu.SemaphoreType.DMA((CHUNKS,))],
        compiler_params=pltpu.CompilerParams(vmem_limit_bytes=61 << 20),
        name="first_part",
    )(waits, momentum, gradients)
    moved = lax.all_to_all(direction, OWNERS, 0, 0, tiled=True)
    iterate = pl.pallas_call(
        whole_matrix,
        out_shape=like,
        in_specs=[in_vmem],
        out_specs=in_vmem,
        scratch_shapes=[pltpu.VMEM((2 * rows, columns), jnp.bfloat16), pltpu.VMEM((rows, columns), jnp.bfloat16)],
        cost_estimate=pl.CostEstimate(flops=6 * 1000 * 1000 * 1000, bytes_accessed=4 << 20, transcendentals=0),
        compiler_params=pltpu.CompilerParams(vmem_limit_bytes=24 << 20),
        name="whole_matrix",
    )(moved)
    back = lax.all_to_all(iterate, OWNERS, 0, 0, tiled=True)
    new_weights, new_momentum = pl.pallas_call(
        last_part,
        out_shape=(like, like),
        in_specs=[in_smem, in_vmem, in_vmem, in_vmem, in_vmem, in_hbm],
        out_specs=(in_hbm, in_hbm),
        scratch_shapes=[held, held, pltpu.SemaphoreType.DMA((2, CHUNKS))],
        input_output_aliases={5: 1},
        compiler_params=pltpu.CompilerParams(vmem_limit_bytes=24 << 20),
        name="last_part",
    )(waits, weights, back, momentum, gradients, new_momentum)
    return by_row(new_weights, shape), by_row(new_momentum, shape)


def solution(mesh):
    spec = P("copy", "fsdp", "tp")
    return jax.shard_map(
        shards, mesh=mesh, in_specs=(spec, spec, spec), out_specs=(spec, spec), check_vma=False
    )
```

time: 150 us -> 119 us (0.79)
  waiting for transfers between devices: 48.3 us -> 0 us
  blocking collectives: 67.7 us -> 89.2 us
  Pallas kernels: 13.2 us -> 29.3 us
  other arithmetic: 12.2 us -> 0 us
  starting transfers between devices: 7.31 us -> 0 us
    all_to_all x1 -> x0, waiting for transfers between devices: 48.3 us -> none  [shards(): back = lax.all_to_all(iterate, OWNERS, 0, 0, tiled=True)]
    all_to_all x0 -> x1, blocking collectives: none -> 40.6 us  [shards(): back = lax.all_to_all(iterate, OWNERS, 0, 0, tiled=True)]
    all_to_all x1, blocking collectives: 67.7 us -> 48.7 us  [shards(): moved = lax.all_to_all(direction, OWNERS, 0, 0, tiled=True)]
    pallas_call x1 -> x3, Pallas kernels: 13.2 us -> 29.3 us  [the longest x1 23 us: shards(): pl.pallas_call(first_part, out_shape=(like, like), in_specs=[in_smem, in_...]
    all_to_all x1 -> x0, starting transfers between devices: 7.31 us -> none  [shards(): back = lax.all_to_all(iterate, OWNERS, 0, 0, tiled=True)]
    add x2 -> x0, other arithmetic: 5.25 us -> none  [the longest x1 4.74 us: shards(): new_momentum = hold_rate * momentum_t + gradients_t]
    mul x1 -> x0, other arithmetic: 3.6 us -> none  [shards(): (1.0 - learn_rate * decay_rate) * weights_t - learn_rate * back]
    sub x1 -> x0, other arithmetic: 3.4 us -> none  [shards(): (1.0 - learn_rate * decay_rate) * weights_t - learn_rate * back]
  transfers between devices with their start and end apart: 1 -> 0, of which waited for: 1 -> 0; matrix products, arithmetic and copies ran while one was open for 2% -> 0% of each run, Pallas kernels for 0% -> 0%
where the time goes in v3:
time: 119 us
  blocking collectives  89.2 us (75%)
  Pallas kernels  29.3 us (25%)
    all_to_all x1, blocking collectives, shards(): moved = lax.all_to_all(direction, OWNERS, 0, 0, tiled=True)  48.7 us
    all_to_all x1, blocking collectives, shards(): back = lax.all_to_all(iterate, OWNERS, 0, 0, tiled=True)  40.6 us
    pallas_call x1, Pallas kernels, shards(): pl.pallas_call(first_part, out_shape=(like, like), in_specs=[in_smem, in_...  23 us
    pallas_call x1, Pallas kernels, shards(): pl.pallas_call(whole_matrix, out_shape=like, in_specs=[in_vmem], out_spec...  4.77 us

profile of v3, /device:TPU:8, one launch (start us, length us, event | category | flops | bytes accessed | tf_op | source)
XLA Modules:
  0.0 119.2 jit_solution(12287218708504401483)
XLA Ops:
  0.6 23.0 %first_part.1 = (f32[128,32,128]{2,1,0:T(8,128)}, f32[128,32,128]{2,1,0:T(8,128)}) custom-call(s32[1]{0:T(128)} %bitcast.waits_ref, f32[128,32,128]{2,1,0:T(8,128)} %bitcast.26, f32[128,32,128]{2,1,0:T(8,128)} %bitcast.28), custom_call_target="tpu_custom_call" | custom-call | tf_op jit(solution)/shard_map/first_part/pallas_call | solution.py:183
  23.7 48.7 %all_to_all.10.x_ref = f32[128,32,128]{2,1,0:T(8,128)S(1)} all-to-all(f32[128,32,128]{2,1,0:T(8,128)} %get-tuple-element.6), channel_id=1, replica_groups=mesh['copy'=2,'fsdp'=32,'tp'=4] {'fsdp','tp'}, dimensions={0} | all-to-all | bytes 4194304 | tf_op jit(solution)/shard_map/all_to_all | solution.py:192
  72.3 0.0 copy-start.2
  72.3 4.8 %whole_matrix.1 = f32[128,32,128]{2,1,0:T(8,128)S(1)} custom-call(f32[128,32,128]{2,1,0:T(8,128)S(1)} %all_to_all.10.x_ref), custom_call_target="tpu_custom_call" | custom-call | flops 6000000000 | bytes 4194304 | tf_op jit(solution)/shard_map/whole_matrix/pallas_call | solution.py:193
  77.1 0.0 copy-start
  77.1 0.0 copy-start.1
  77.1 40.6 %all_to_all.11.back_ref = f32[128,32,128]{2,1,0:T(8,128)S(1)} all-to-all(f32[128,32,128]{2,1,0:T(8,128)S(1)} %whole_matrix.1), channel_id=1, replica_groups=mesh['copy'=2,'fsdp'=32,'tp'=4] {'fsdp','tp'}, dimensions={0} | all-to-all | bytes 4194304 | tf_op jit(solution)/shard_map/all_to_all | solution.py:203
  117.7 0.0 copy-done.2
  117.7 0.0 copy-done
  117.7 0.0 copy-done.1
  117.7 1.5 %last_part.1 = (f32[128,32,128]{2,1,0:T(8,128)}, f32[128,32,128]{2,1,0:T(8,128)}) custom-call(s32[1]{0:T(128)} %bitcast.waits_ref, f32[128,32,128]{2,1,0:T(8,128)S(1)} %bitcast.30, f32[128,32,128]{2,1,0:T(8,128)S(1)} %all_to_all.11.back_ref, f32[128,32,128]{2,1,0:T(8,128)S(1)} %bitcast.27, ...), custom_call_target="tpu_custom_call", output_to_operand_aliasing={{1}: (5, {})} | custom-call | tf_op jit(solution)/shard_map/last_part/pallas_call | solution.py:204
Async XLA Ops:
  72.3 45.4 %copy-start.2 = (f32[128,4,1024]{2,1,0:T(4,128)S(1)}, f32[128,4,1024]{2,1,0:T(4,128)}, u32[]{:S(2)}) copy-start(f32[128,4,1024]{2,1,0:T(4,128)} %param.5) | copy-start | bytes 6291460
  77.1 40.6 %copy-start = (f32[128,4,1024]{2,1,0:T(4,128)S(1)}, f32[128,4,1024]{2,1,0:T(4,128)}, u32[]{:S(2)}) copy-start(f32[128,4,1024]{2,1,0:T(4,128)} %param.4) | copy-start | bytes 6291460
  77.1 40.6 %copy-start.1 = (f32[128,4,1024]{2,1,0:T(4,128)S(1)}, f32[128,4,1024]{2,1,0:T(4,128)}, u32[]{:S(2)}) copy-start(f32[128,4,1024]{2,1,0:T(4,128)} %param.3) | copy-start | bytes 6291460

commit v4 on v3

--- a/solution.py
+++ b/solution.py
@@ -186,7 +186,7 @@
         in_specs=[in_smem, in_hbm, in_hbm],
         out_specs=(in_vmem, in_hbm),
         scratch_shapes=[held, held, held, pltpu.SemaphoreType.DMA((2, CHUNKS)), pltpu.SemaphoreType.DMA((CHUNKS,))],
-        compiler_params=pltpu.CompilerParams(vmem_limit_bytes=61 << 20),
+        compiler_params=pltpu.CompilerParams(vmem_limit_bytes=50 << 20),
         name="first_part",
     )(waits, momentum, gradients)
     moved = lax.all_to_all(direction, OWNERS, 0, 0, tiled=True)

time: 119 us -> 118 us (level)
  Pallas kernels: 29.3 us -> 28 us
    pallas_call x1, Pallas kernels: 23 us -> 21.7 us  [shards(): pl.pallas_call(first_part, out_shape=(like, like), in_specs=[in_smem, in_...]
where the time goes in v4:
time: 118 us
  blocking collectives  89 us (75%)
  Pallas kernels  28 us (24%)
    all_to_all x1, blocking collectives, shards(): moved = lax.all_to_all(direction, OWNERS, 0, 0, tiled=True)  48.4 us
    all_to_all x1, blocking collectives, shards(): back = lax.all_to_all(iterate, OWNERS, 0, 0, tiled=True)  40.6 us
    pallas_call x1, Pallas kernels, shards(): pl.pallas_call(first_part, out_shape=(like, like), in_specs=[in_smem, in_...  21.7 us
    pallas_call x1, Pallas kernels, shards(): pl.pallas_call(whole_matrix, out_shape=like, in_specs=[in_vmem], out_spec...  4.77 us

profile of v4, /device:TPU:8, one launch (start us, length us, event | category | flops | bytes accessed | tf_op | source)
XLA Modules:
  0.0 117.7 jit_solution(7192962887537979768)
XLA Ops:
  0.6 21.7 %first_part.1 = (f32[128,32,128]{2,1,0:T(8,128)S(1)}, f32[128,32,128]{2,1,0:T(8,128)}) custom-call(s32[1]{0:T(128)} %bitcast.waits_ref, f32[128,32,128]{2,1,0:T(8,128)} %bitcast.26, f32[128,32,128]{2,1,0:T(8,128)} %bitcast.28), custom_call_target="tpu_custom_call" | custom-call | tf_op jit(solution)/shard_map/first_part/pallas_call | solution.py:183
  22.4 48.4 %all_to_all.10.x_ref = f32[128,32,128]{2,1,0:T(8,128)S(1)} all-to-all(f32[128,32,128]{2,1,0:T(8,128)S(1)} %get-tuple-element.6), channel_id=1, replica_groups=mesh['copy'=2,'fsdp'=32,'tp'=4] {'fsdp','tp'}, dimensions={0} | all-to-all | bytes 4194304 | tf_op jit(solution)/shard_map/all_to_all | solution.py:192
  70.8 0.0 copy-start.2
  70.8 4.8 %whole_matrix.1 = f32[128,32,128]{2,1,0:T(8,128)S(1)} custom-call(f32[128,32,128]{2,1,0:T(8,128)S(1)} %all_to_all.10.x_ref), custom_call_target="tpu_custom_call" | custom-call | flops 6000000000 | bytes 4194304 | tf_op jit(solution)/shard_map/whole_matrix/pallas_call | solution.py:193
  75.6 0.0 copy-start
  75.6 0.0 copy-start.1
  75.6 40.6 %all_to_all.11.back_ref = f32[128,32,128]{2,1,0:T(8,128)S(1)} all-to-all(f32[128,32,128]{2,1,0:T(8,128)S(1)} %whole_matrix.1), channel_id=1, replica_groups=mesh['copy'=2,'fsdp'=32,'tp'=4] {'fsdp','tp'}, dimensions={0} | all-to-all | bytes 4194304 | tf_op jit(solution)/shard_map/all_to_all | solution.py:203
  116.2 0.0 copy-done.2
  116.2 0.0 copy-done
  116.2 0.0 copy-done.1
  116.2 1.5 %last_part.1 = (f32[128,32,128]{2,1,0:T(8,128)}, f32[128,32,128]{2,1,0:T(8,128)}) custom-call(s32[1]{0:T(128)} %bitcast.waits_ref, f32[128,32,128]{2,1,0:T(8,128)S(1)} %bitcast.30, f32[128,32,128]{2,1,0:T(8,128)S(1)} %all_to_all.11.back_ref, f32[128,32,128]{2,1,0:T(8,128)S(1)} %bitcast.27, ...), custom_call_target="tpu_custom_call", output_to_operand_aliasing={{1}: (5, {})} | custom-call | tf_op jit(solution)/shard_map/last_part/pallas_call | solution.py:204
Async XLA Ops:
  70.8 45.4 %copy-start.2 = (f32[128,4,1024]{2,1,0:T(4,128)S(1)}, f32[128,4,1024]{2,1,0:T(4,128)}, u32[]{:S(2)}) copy-start(f32[128,4,1024]{2,1,0:T(4,128)} %param.5) | copy-start | bytes 6291460
  75.6 40.6 %copy-start = (f32[128,4,1024]{2,1,0:T(4,128)S(1)}, f32[128,4,1024]{2,1,0:T(4,128)}, u32[]{:S(2)}) copy-start(f32[128,4,1024]{2,1,0:T(4,128)} %param.4) | copy-start | bytes 6291460
  75.6 40.6 %copy-start.1 = (f32[128,4,1024]{2,1,0:T(4,128)S(1)}, f32[128,4,1024]{2,1,0:T(4,128)}, u32[]{:S(2)}) copy-start(f32[128,4,1024]{2,1,0:T(4,128)} %param.3) | copy-start | bytes 6291460

commit v5 on v4

--- a/solution.py
+++ b/solution.py
@@ -11,6 +11,10 @@
 decay_rate = 0.1
 LINEAR, CUBIC, QUINTIC = 3.4445, -4.775, 2.0315
 OWNERS = ("fsdp", "tp")
+TPS, HEIGHT, DEPTH = 4, 8, 4
+FAR_FIRST = [z // 2 + HEIGHT // 2 * (z % 2) for z in range(HEIGHT)]
+ORDER = [(z * DEPTH + y) * TPS + x for x in range(TPS) for y in range(DEPTH) for z in FAR_FIRST]
+PLACES = [sorted((i for i, d in enumerate(ORDER) if d % TPS == t), key=lambda i: ORDER[i]) for t in range(TPS)]
 TURN_NANOS = 18000
 
 
@@ -42,7 +46,11 @@
 
 
 def product(a, b):
-    return times(left_factors(a), *pieces(b))
+    (ah, am, al), (bh, bm, bl) = a, b
+    side = ah.shape[0]
+    upper = jnp.concatenate([bh, bm], axis=0)
+    both = dot(jnp.concatenate([ah, am], axis=1), jnp.concatenate([upper, jnp.concatenate([bl, bh], axis=0)], axis=1))
+    return both[:, :side] + (both[:, side:] + dot(jnp.concatenate([al, ah], axis=1), upper))
 
 
 def whole_matrix(x_ref, y_ref, main_ref, low_ref):
@@ -50,8 +58,6 @@
     rows = low_ref.shape[0]
     tps = sources * 4 // rows
     fsdps = sources // tps
-    view = x_ref.reshape(fsdps, tps, lines, lanes)
-    out = y_ref.reshape(fsdps, tps, lines, lanes)
     upper = lax.broadcasted_iota(jnp.int32, (fsdps // 2, 8, lanes), 1) < 4
     places = [(t, p, (t * (lines // 8) + p) * 2 * lanes) for t in range(tps) for p in range(lines // 8)]
 
@@ -59,8 +65,8 @@
         return jnp.where(upper, a, pltpu.roll(b, 4, 1)), jnp.where(upper, pltpu.roll(a, 4, 1), b)
 
     def columns(t, p):
-        z = view[:, t, p * 8 : p * 8 + 8, :].reshape(fsdps // 2, 2, 8, lanes)
-        left, right = cross(z[:, 0], z[:, 1])
+        a, b = (jnp.stack([x_ref[i, p * 8 : p * 8 + 8, :] for i in PLACES[t][k::2]]) for k in range(2))
+        left, right = cross(a, b)
         return jnp.concatenate([left.reshape(rows, lanes), right.reshape(rows, lanes)], axis=1)
 
     for t, p, c in places:
@@ -81,11 +87,12 @@
     gram = gram / total
     applied = None
     for step in range(ITERS):
-        factors = left_factors(gram)
-        extra = (CUBIC / LINEAR) * gram + (QUINTIC / LINEAR) * times(factors, *pieces(gram))
-        applied = extra if applied is None else applied + (extra + product(extra, applied))
+        powers = pieces(gram)
+        extra = (CUBIC / LINEAR) * gram + (QUINTIC / LINEAR) * product(powers, powers)
+        more = pieces(extra)
         if step < ITERS - 1:
-            gram = LINEAR**2 * (gram + times(factors, *pieces(2.0 * extra + product(extra, extra))))
+            gram = LINEAR**2 * (gram + product(powers, pieces(2.0 * extra + product(more, more))))
+        applied = extra if applied is None else applied + (extra + product(more, pieces(applied)))
     scale = learn_rate * LINEAR**ITERS * lax.rsqrt(total)
     factors = left_factors(applied)
     for t, p, c in places:
@@ -93,8 +100,9 @@
         y = scale * (columns(t, p) + times(factors, main_ref[:rows, span], main_ref[rows:, span], low_ref[:, span]))
         left, right = (y[:, :lanes].reshape(fsdps // 2, 8, lanes), y[:, lanes:].reshape(fsdps // 2, 8, lanes))
         a, b = cross(left, right)
-        z = jnp.concatenate([a[:, None], b[:, None]], axis=1).reshape(fsdps, 8, lanes)
-        out[:, t, p * 8 : p * 8 + 8, :] = z
+        for k, half in enumerate((a, b)):
+            for n, i in enumerate(PLACES[t][k::2]):
+                y_ref[i, p * 8 : p * 8 + 8, :] = half[n]
 
 
 CHUNKS = 8
@@ -189,7 +197,7 @@
         compiler_params=pltpu.CompilerParams(vmem_limit_bytes=50 << 20),
         name="first_part",
     )(waits, momentum, gradients)
-    moved = lax.all_to_all(direction, OWNERS, 0, 0, tiled=True)
+    moved = lax.all_to_all(direction, OWNERS, 0, 0, tiled=True, axis_index_groups=[ORDER])
     iterate = pl.pallas_call(
         whole_matrix,
         out_shape=like,
@@ -200,7 +208,7 @@
         compiler_params=pltpu.CompilerParams(vmem_limit_bytes=24 << 20),
         name="whole_matrix",
     )(moved)
-    back = lax.all_to_all(iterate, OWNERS, 0, 0, tiled=True)
+    back = lax.all_to_all(iterate, OWNERS, 0, 0, tiled=True, axis_index_groups=[ORDER])
     new_weights, new_momentum = pl.pallas_call(
         last_part,
         out_shape=(like, like),

time: 118 us -> 117 us (level)
  blocking collectives: 89 us -> 87.8 us
where the time goes in v5:
time: 117 us; the launch traced here: 116 us
  blocking collectives  87.8 us (75%)
  Pallas kernels  27.8 us (24%)
    all_to_all x1, blocking collectives, shards(): lax.all_to_all(direction, OWNERS, 0, 0, tiled=True, axis_index_groups=[OR...  47 us
    all_to_all x1, blocking collectives, shards(): lax.all_to_all(iterate, OWNERS, 0, 0, tiled=True, axis_index_groups=[ORDER])  40.9 us
    pallas_call x1, Pallas kernels, shards(): pl.pallas_call(first_part, out_shape=(like, like), in_specs=[in_smem, in_...  21.7 us
    pallas_call x1, Pallas kernels, shards(): pl.pallas_call(whole_matrix, out_shape=like, in_specs=[in_vmem], out_spec...  4.56 us

profile of v5, /device:TPU:8, one launch (start us, length us, event | category | flops | bytes accessed | tf_op | source)
XLA Modules:
  0.0 116.3 jit_solution(8525976418648713884)
XLA Ops:
  0.6 21.7 %first_part.1 = (f32[128,32,128]{2,1,0:T(8,128)S(1)}, f32[128,32,128]{2,1,0:T(8,128)}) custom-call(s32[1]{0:T(128)} %bitcast.waits_ref, f32[128,32,128]{2,1,0:T(8,128)} %bitcast.26, f32[128,32,128]{2,1,0:T(8,128)} %bitcast.28), custom_call_target="tpu_custom_call" | custom-call | tf_op jit(solution)/shard_map/first_part/pallas_call | solution.py:191
  22.4 47.0 %all_to_all.10.x_ref = f32[128,32,128]{2,1,0:T(8,128)S(1)} all-to-all(f32[128,32,128]{2,1,0:T(8,128)S(1)} %get-tuple-element.6), channel_id=1, replica_groups={{0,64,16,80,32,96,48,112,4,68,20,84,36,100,52,116,8,72,24,88,40,104,56,..., dimensions={0} | all-to-all | bytes 4194304 | tf_op jit(solution)/shard_map/all_to_all | solution.py:200
  69.4 0.0 copy-start.2
  69.4 4.6 %whole_matrix.1 = f32[128,32,128]{2,1,0:T(8,128)S(1)} custom-call(f32[128,32,128]{2,1,0:T(8,128)S(1)} %all_to_all.10.x_ref), custom_call_target="tpu_custom_call" | custom-call | flops 6000000000 | bytes 4194304 | tf_op jit(solution)/shard_map/whole_matrix/pallas_call | solution.py:201
  73.9 0.0 copy-start
  73.9 0.0 copy-start.1
  74.0 40.9 %all_to_all.11.back_ref = f32[128,32,128]{2,1,0:T(8,128)S(1)} all-to-all(f32[128,32,128]{2,1,0:T(8,128)S(1)} %whole_matrix.1), channel_id=1, replica_groups={{0,64,16,80,32,96,48,112,4,68,20,84,36,100,52,116,8,72,24,88,40,104,56,..., dimensions={0} | all-to-all | bytes 4194304 | tf_op jit(solution)/shard_map/all_to_all | solution.py:211
  114.8 0.0 copy-done.2
  114.8 0.0 copy-done
  114.8 0.0 copy-done.1
  114.8 1.5 %last_part.1 = (f32[128,32,128]{2,1,0:T(8,128)}, f32[128,32,128]{2,1,0:T(8,128)}) custom-call(s32[1]{0:T(128)} %bitcast.waits_ref, f32[128,32,128]{2,1,0:T(8,128)S(1)} %bitcast.30, f32[128,32,128]{2,1,0:T(8,128)S(1)} %all_to_all.11.back_ref, f32[128,32,128]{2,1,0:T(8,128)S(1)} %bitcast.27, ...), custom_call_target="tpu_custom_call", output_to_operand_aliasing={{1}: (5, {})} | custom-call | tf_op jit(solution)/shard_map/last_part/pallas_call | solution.py:212
Async XLA Ops:
  69.4 45.4 %copy-start.2 = (f32[128,4,1024]{2,1,0:T(4,128)S(1)}, f32[128,4,1024]{2,1,0:T(4,128)}, u32[]{:S(2)}) copy-start(f32[128,4,1024]{2,1,0:T(4,128)} %param.5) | copy-start | bytes 6291460
  73.9 40.9 %copy-start = (f32[128,4,1024]{2,1,0:T(4,128)S(1)}, f32[128,4,1024]{2,1,0:T(4,128)}, u32[]{:S(2)}) copy-start(f32[128,4,1024]{2,1,0:T(4,128)} %param.4) | copy-start | bytes 6291460
  73.9 40.9 %copy-start.1 = (f32[128,4,1024]{2,1,0:T(4,128)S(1)}, f32[128,4,1024]{2,1,0:T(4,128)}, u32[]{:S(2)}) copy-start(f32[128,4,1024]{2,1,0:T(4,128)} %param.3) | copy-start | bytes 6291460

commit v6 on v5

--- a/solution.py
+++ b/solution.py
@@ -84,11 +84,14 @@
     i = lax.broadcasted_iota(jnp.int32, (rows, rows), 0)
     j = lax.broadcasted_iota(jnp.int32, (rows, rows), 1)
     total = jnp.sum(jnp.sum(jnp.where(i == j, gram, 0.0), axis=1, keepdims=True), axis=0, keepdims=True) + 1e-06
-    gram = gram / total
+    raw = pieces(gram)
+    inverse = 1.0 / total
+    square = product(raw, raw) * (inverse * inverse)
+    gram = gram * inverse
     applied = None
     for step in range(ITERS):
         powers = pieces(gram)
-        extra = (CUBIC / LINEAR) * gram + (QUINTIC / LINEAR) * product(powers, powers)
+        extra = (CUBIC / LINEAR) * gram + (QUINTIC / LINEAR) * (square if step == 0 else product(powers, powers))
         more = pieces(extra)
         if step < ITERS - 1:
             gram = LINEAR**2 * (gram + product(powers, pieces(2.0 * extra + product(more, more))))

time: 117 us -> 117 us (level)
  no operation moved by 1% of the time
where the time goes in v6:
time: 117 us; the launch traced here: 116 us
  blocking collectives  87.7 us (75%)
  Pallas kernels  27.7 us (24%)
    all_to_all x1, blocking collectives, shards(): lax.all_to_all(direction, OWNERS, 0, 0, tiled=True, axis_index_groups=[OR...  46.9 us
    all_to_all x1, blocking collectives, shards(): lax.all_to_all(iterate, OWNERS, 0, 0, tiled=True, axis_index_groups=[ORDER])  40.8 us
    pallas_call x1, Pallas kernels, shards(): pl.pallas_call(first_part, out_shape=(like, like), in_specs=[in_smem, in_...  21.7 us
    pallas_call x1, Pallas kernels, shards(): pl.pallas_call(whole_matrix, out_shape=like, in_specs=[in_vmem], out_spec...  4.46 us

profile of v6, /device:TPU:8, one launch (start us, length us, event | category | flops | bytes accessed | tf_op | source)
XLA Modules:
  0.0 116.1 jit_solution(101394239865964913)
XLA Ops:
  0.6 21.7 %first_part.1 = (f32[128,32,128]{2,1,0:T(8,128)S(1)}, f32[128,32,128]{2,1,0:T(8,128)}) custom-call(s32[1]{0:T(128)} %bitcast.waits_ref, f32[128,32,128]{2,1,0:T(8,128)} %bitcast.26, f32[128,32,128]{2,1,0:T(8,128)} %bitcast.28), custom_call_target="tpu_custom_call" | custom-call | tf_op jit(solution)/shard_map/first_part/pallas_call | solution.py:194
  22.4 46.9 %all_to_all.10.x_ref = f32[128,32,128]{2,1,0:T(8,128)S(1)} all-to-all(f32[128,32,128]{2,1,0:T(8,128)S(1)} %get-tuple-element.6), channel_id=1, replica_groups={{0,64,16,80,32,96,48,112,4,68,20,84,36,100,52,116,8,72,24,88,40,104,56,..., dimensions={0} | all-to-all | bytes 4194304 | tf_op jit(solution)/shard_map/all_to_all | solution.py:203
  69.3 0.0 copy-start.2
  69.3 4.5 %whole_matrix.1 = f32[128,32,128]{2,1,0:T(8,128)S(1)} custom-call(f32[128,32,128]{2,1,0:T(8,128)S(1)} %all_to_all.10.x_ref), custom_call_target="tpu_custom_call" | custom-call | flops 6000000000 | bytes 4194304 | tf_op jit(solution)/shard_map/whole_matrix/pallas_call | solution.py:204
  73.8 0.0 copy-start
  73.8 0.0 copy-start.1
  73.8 40.8 %all_to_all.11.back_ref = f32[128,32,128]{2,1,0:T(8,128)S(1)} all-to-all(f32[128,32,128]{2,1,0:T(8,128)S(1)} %whole_matrix.1), channel_id=1, replica_groups={{0,64,16,80,32,96,48,112,4,68,20,84,36,100,52,116,8,72,24,88,40,104,56,..., dimensions={0} | all-to-all | bytes 4194304 | tf_op jit(solution)/shard_map/all_to_all | solution.py:214
  114.6 0.0 copy-done.2
  114.6 0.0 copy-done
  114.6 0.0 copy-done.1
  114.6 1.5 %last_part.1 = (f32[128,32,128]{2,1,0:T(8,128)}, f32[128,32,128]{2,1,0:T(8,128)}) custom-call(s32[1]{0:T(128)} %bitcast.waits_ref, f32[128,32,128]{2,1,0:T(8,128)S(1)} %bitcast.30, f32[128,32,128]{2,1,0:T(8,128)S(1)} %all_to_all.11.back_ref, f32[128,32,128]{2,1,0:T(8,128)S(1)} %bitcast.27, ...), custom_call_target="tpu_custom_call", output_to_operand_aliasing={{1}: (5, {})} | custom-call | tf_op jit(solution)/shard_map/last_part/pallas_call | solution.py:215
Async XLA Ops:
  69.3 45.3 %copy-start.2 = (f32[128,4,1024]{2,1,0:T(4,128)S(1)}, f32[128,4,1024]{2,1,0:T(4,128)}, u32[]{:S(2)}) copy-start(f32[128,4,1024]{2,1,0:T(4,128)} %param.5) | copy-start | bytes 6291460
  73.8 40.8 %copy-start = (f32[128,4,1024]{2,1,0:T(4,128)S(1)}, f32[128,4,1024]{2,1,0:T(4,128)}, u32[]{:S(2)}) copy-start(f32[128,4,1024]{2,1,0:T(4,128)} %param.4) | copy-start | bytes 6291460
  73.8 40.8 %copy-start.1 = (f32[128,4,1024]{2,1,0:T(4,128)S(1)}, f32[128,4,1024]{2,1,0:T(4,128)}, u32[]{:S(2)}) copy-start(f32[128,4,1024]{2,1,0:T(4,128)} %param.3) | copy-start | bytes 6291460
